TPU v7x, 768 devices: a whole 4x8x12 slice. The times are simulated.
768 devices in a mesh: aa: 6 (over z_hi, core), ba: 128 (over z_lo, y, x).
Axes of the slice: x: 4, y: 8, z: 12 (z_hi: 3, z_lo: 4; z = z_hi * 4 + z_lo), core: 2. Of those that a mesh axis runs over, the one named last changes fastest.
Arguments:
- queries: bfloat16 [6, 128, 192, 1024], P('aa', 'ba'), may hold values from -6 to 6
- key_rows: bfloat16 [6, 128, 192, 1024], P('aa', 'ba'), may hold values from -6 to 6
- value_rows: bfloat16 [6, 128, 192, 1024], P('aa', 'ba'), may hold values from -24 to 24
- out_proj: bfloat16 [6, 1024, 1024], P('aa', 'ba'), may hold values from -0.1875 to 0.1875
- scale_ids: int32 [128, 192], P('ba'), may hold values from 0 to 7, never falling along the last dimension, each value on 1 to 64 neighbouring positions
- residual_in: bfloat16 [128, 192, 1024], P('ba'), may hold values from -4 to 4
- cotangent: bfloat16 [128, 192, 1024], P('ba'), may hold values from -6 to 6
Outputs:
- residual_out: bfloat16 [6, 128, 192, 1024], P('aa', 'ba')
- grad_query: bfloat16 [6, 128, 192, 1024], P('aa', 'ba')
- grad_key: bfloat16 [6, 128, 192, 1024], P('aa', 'ba')
- grad_value: bfloat16 [6, 128, 192, 1024], P('aa', 'ba')
- grad_proj: float32 [6, 1024, 1024], P('aa', 'ba')
Inputs may be any that keep to these rules, and one draw needn't show every extreme that they name: `scale_ids`: for each image the scale ids never fall along the tokens; every scale from 0 to 7 is present, with 1 to 64 tokens.
All inputs are finite; a program needn't handle non-finite values.
Results may differ from a plain program's by a relative error of at most 0.0086.
Values may be sent and summed in bfloat16 or wider, within the bound.
A program may use at most 64 MiB of HBM per device.

v0:
```python
import jax
import jax.numpy as jnp
from jax import lax
from jax.sharding import Mesh
from jax.sharding import PartitionSpec as P

HD = 64
BA = ("ba_0", "ba_1", "ba_2")


def joined_along(tiles, dim):
    tiles = jnp.moveaxis(tiles, 0, dim)
    shape = tiles.shape
    return tiles.reshape(*shape[:dim], shape[dim] * shape[dim + 1], *shape[dim + 2 :])


def stacked_from(value, axes, turns):
    tiles = value
    for k in turns:
        tiles = lax.all_gather(tiles, axes[k])
    done = turns[::-1]
    back = [done.index(k) for k in range(len(axes))]
    tiles = tiles.transpose(*back, *range(len(axes), tiles.ndim))
    return tiles.reshape(-1, *value.shape)


def gather_axes(value, axes, turns, dim):
    return joined_along(stacked_from(value, axes, turns), dim)


def passed_along(value, axis, by):
    devices = lax.axis_size(axis)
    pairs = [(i, i + by) for i in range(devices) if 0 <= i + by < devices]
    return lax.ppermute(value, axis, pairs)


def cut_along(value, dim, devices):
    shape = value.shape
    tiles = value.reshape(*shape[:dim], devices, shape[dim] // devices, *shape[dim + 1 :])
    return jnp.moveaxis(tiles, dim, 0)


def scatter_lines(value, axis, dim):
    devices = lax.axis_size(axis)
    tiles = cut_along(value, dim, devices)
    length = value.size // devices
    spare = max(2048 - length, -length % 1024)
    padded = jnp.pad(tiles.reshape(devices, length), ((0, 0), (0, spare)))
    own = lax.psum_scatter(padded.reshape(-1, 128), axis, scatter_dimension=0, tiled=True)
    return own.reshape(-1)[:length].reshape(tiles.shape[1:])


def local(queries, key_rows, value_rows, out_proj, scale_ids, residual_in, cotangent):
    images = queries.shape[1]
    length = queries.shape[2]
    inner_width = queries.shape[3]
    head_count = inner_width // HD
    res_width = residual_in.shape[2]
    flat_rows = images * length
    score_scale = HD ** (-0.5)
    image_weight = 1.0 / (lax.axis_size(BA) * images)
    w_full = gather_axes(out_proj, BA, (0, 1, 2), 1)[0]
    visible = scale_ids[:, None, :] <= scale_ids[:, :, None]
    q_heads = queries[0].reshape(images, length, head_count, HD)
    k_heads = key_rows[0].reshape(images, length, head_count, HD)
    v_heads = value_rows[0].reshape(images, length, head_count, HD)
    scores = (
        jnp.einsum("bihd,bjhd->bhij", q_heads, k_heads, preferred_element_type=jnp.float32)
        * score_scale
    )
    scores = jnp.where(visible[:, None], scores, -jnp.inf)
    row_max = jnp.max(scores, axis=-1, keepdims=True)
    lifted = jnp.exp(scores - row_max)
    attn_probs = lifted / jnp.sum(lifted, axis=-1, keepdims=True)
    probs_low = attn_probs.astype(jnp.bfloat16)
    attended = jnp.einsum("bhij,bjhd->bihd", probs_low, v_heads, preferred_element_type=jnp.float32)
    attn_rows = attended.astype(jnp.bfloat16).reshape(flat_rows, inner_width)
    branch = jnp.dot(attn_rows, w_full, preferred_element_type=jnp.float32)

    def relay_step(hop_index, running):
        return branch + passed_along(running, "aa", 1)

    carried = lax.fori_loop(0, lax.axis_size("aa") - 1, relay_step, branch)
    residual_rows = residual_in.reshape(flat_rows, res_width).astype(jnp.float32) + carried
    residual_out = residual_rows.astype(jnp.bfloat16).reshape(images, length, res_width)
    cot_rows = cotangent.reshape(flat_rows, res_width)
    d_attn = lax.dot_general(
        cot_rows, w_full, (((1,), (1,)), ((), ())), preferred_element_type=jnp.float32
    ).astype(jnp.bfloat16)
    product = lax.dot_general(
        attn_rows, cot_rows, (((0,), (0,)), ((), ())), preferred_element_type=jnp.float32
    )
    grad_proj = scatter_lines(product * image_weight, BA, 0)
    d_heads = d_attn.reshape(images, length, head_count, HD)
    grad_value = jnp.einsum(
        "bhij,bihd->bjhd", probs_low, d_heads, preferred_element_type=jnp.float32
    )
    d_probs = jnp.einsum("bihd,bjhd->bhij", d_heads, v_heads, preferred_element_type=jnp.float32)
    row_delta = jnp.sum(attn_probs * d_probs, axis=-1, keepdims=True)
    d_scores = (attn_probs * (d_probs - row_delta) * score_scale).astype(jnp.bfloat16)
    grad_query = jnp.einsum(
        "bhij,bjhd->bihd", d_scores, k_heads, preferred_element_type=jnp.float32
    )
    grad_key = jnp.einsum("bhij,bihd->bjhd", d_scores, q_heads, preferred_element_type=jnp.float32)
    return (
        residual_out[None],
        grad_query.reshape(images, length, inner_width).astype(jnp.bfloat16)[None],
        grad_key.reshape(images, length, inner_width).astype(jnp.bfloat16)[None],
        grad_value.reshape(images, length, inner_width).astype(jnp.bfloat16)[None],
        grad_proj[None],
    )


def solution(mesh):
    torus = Mesh(mesh.devices.reshape(mesh.shape["aa"], 4, 8, 4), ("aa", "ba_0", "ba_1", "ba_2"))
    return jax.shard_map(
        local,
        mesh=torus,
        in_specs=(
            P("aa", BA, None, None),
            P("aa", BA, None, None),
            P("aa", BA, None, None),
            P("aa", BA, None),
            P(BA, None),
            P(BA, None, None),
            P(BA, None, None),
        ),
        out_specs=(
            P("aa", BA, None, None),
            P("aa", BA, None, None),
            P("aa", BA, None, None),
            P("aa", BA, None, None),
            P("aa", BA, None),
        ),
        check_vma=False,
    )
```

profile of v0, /device:TPU:256, one launch (start us, length us, event | category | flops | bytes accessed | tf_op | source)
XLA Modules:
  0.0 923.4 jit_solution(12139827054598204055)
XLA Ops:
  8.1 15.4 %all-gather = bf16[4,8,1024]{2,1,0:T(8,128)(2,1)S(1)} all-gather(bf16[1,8,1024]{2,1,0:T(8,128)(2,1)} %param.12), channel_id=2, replica_groups=mesh['aa'=6,'ba_0'=4,'ba_1'=8,'ba_2'=4] {'ba_0'}, dimensions={0}, use_global_device_ids=true | all-gather | bytes 81920 | tf_op jit(solution)/shard_map/all_gather | solution.py:20
  23.5 28.9 %all-gather.1 = bf16[32,8,1024]{2,1,0:T(8,128)(2,1)} all-gather(bf16[4,8,1024]{2,1,0:T(8,128)(2,1)S(1)} %all-gather), channel_id=3, replica_groups=mesh['aa'=6,'ba_0'=4,'ba_1'=8,'ba_2'=4] {'ba_1'}, dimensions={0}, use_global_device_ids=true | all-gather | bytes 589824 | tf_op jit(solution)/shard_map/all_gather | solution.py:20
  55.5 3.0 fusion.37
  58.5 3.1 convolution_convert_fusion
  61.6 3.7 convolution_multiply_fusion
  65.3 4.9 reshape.187
  70.2 21.6 %all-gather.5.cloned.1.call-done = bf16[32,4,1,8,1024]{4,3,2,1,0:T(8,128)(2,1)} async-done(((bf16[8,4,1,8,1024]{4,3,2,1,0:T(8,128)(2,1)}), bf16[32,4,1,8,1024]{4,3,2,1,0:T(8,128)(2,1)}) %all-gather.5.cloned.1.call-update) | async-done | bytes 2097168 | tf_op jit(solution)/shard_map/all_gather | solution.py:20
  96.4 3.5 convolution_convert_fusion.1
  99.9 2.0 copy.62
  103.7 3.4 fusion.39
  107.1 6.8 fusion.20
  113.9 2.0 copy.61
  115.9 6.0 fusion.17
  122.8 156.2 %while.10 = (s32[]{:T(128)}, f32[192,1024]{1,0:T(8,128)S(1)}, f32[192,1024]{1,0:T(8,128)S(1)}, s32[]{:T(128)}) while((s32[]{:T(128)}, f32[192,1024]{1,0:T(8,128)S(1)}, f32[192,1024]{1,0:T(8,128)S(1)}, s32[]{:T(128)}) %tuple.27), condition=%wide.region_3.4_spmd, body=%wide.region_2.3_spmd.sunk | while | flops 196610 | bytes 5505117 | solution.py:83
  122.8 2.0 collective-permute-start
  124.9 16.2 %collective-permute-done = f32[192,1024]{1,0:T(8,128)S(1)} collective-permute-done((f32[192,1024]{1,0:T(8,128)S(1)}, f32[192,1024]{1,0:T(8,128)S(1)}, u32[]{:S(2)}, u32[]{:S(2)}) %collective-permute-start) | collective-permute-done | bytes 786464 | tf_op jit(solution)/shard_map/while/body/eval_jaxpr/ppermute | solution.py:34
  141.2 1.9 collective-permute-start
  143.1 15.7 %collective-permute-done = f32[192,1024]{1,0:T(8,128)S(1)} collective-permute-done((f32[192,1024]{1,0:T(8,128)S(1)}, f32[192,1024]{1,0:T(8,128)S(1)}, u32[]{:S(2)}, u32[]{:S(2)}) %collective-permute-start) | collective-permute-done | bytes 786464 | tf_op jit(solution)/shard_map/while/body/eval_jaxpr/ppermute | solution.py:34
  159.0 11.4 %collective-permute-start = (f32[192,1024]{1,0:T(8,128)S(1)}, f32[192,1024]{1,0:T(8,128)S(1)}, u32[]{:S(2)}, u32[]{:S(2)}) collective-permute-start(f32[192,1024]{1,0:T(8,128)S(1)} %get-tuple-element.75), channel_id=1, source_target_pairs={{0,128},{128,256},{256,384},{384,512},{512,640},{1,129},{129,257},... | collective-permute-start | bytes 2359304 | tf_op jit(solution)/shard_map/while/body/eval_jaxpr/ppermute | solution.py:34
  170.4 6.5 collective-permute-done
  177.0 66.9 %collective-permute-start = (f32[192,1024]{1,0:T(8,128)S(1)}, f32[192,1024]{1,0:T(8,128)S(1)}, u32[]{:S(2)}, u32[]{:S(2)}) collective-permute-start(f32[192,1024]{1,0:T(8,128)S(1)} %get-tuple-element.75), channel_id=1, source_target_pairs={{0,128},{128,256},{256,384},{384,512},{512,640},{1,129},{129,257},... | collective-permute-start | bytes 2359304 | tf_op jit(solution)/shard_map/while/body/eval_jaxpr/ppermute | solution.py:34
  243.9 1.9 collective-permute-done
  245.9 31.0 %collective-permute-start = (f32[192,1024]{1,0:T(8,128)S(1)}, f32[192,1024]{1,0:T(8,128)S(1)}, u32[]{:S(2)}, u32[]{:S(2)}) collective-permute-start(f32[192,1024]{1,0:T(8,128)S(1)} %get-tuple-element.75), channel_id=1, source_target_pairs={{0,128},{128,256},{256,384},{384,512},{512,640},{1,129},{129,257},... | collective-permute-start | bytes 2359304 | tf_op jit(solution)/shard_map/while/body/eval_jaxpr/ppermute | solution.py:34
  279.8 634.7 %reduce-scatter.2.cloned.1.call-done = f32[64,128]{1,0:T(8,128)} async-done(((f32[8192,128]{1,0:T(8,128)}), f32[64,128]{1,0:T(8,128)}) %reduce-scatter.2.cloned.1.call-update) | async-done | bytes 32784 | tf_op jit(solution)/shard_map/reduce_scatter | solution.py:49
  (44 shorter events, 15.0 us)
Async XLA Ops:
  8.0 53.6 %copy-start = (bf16[1,192,1024]{2,1,0:T(8,128)(2,1)S(1)}, bf16[1,192,1024]{2,1,0:T(8,128)(2,1)}, u32[]{:S(2)}) copy-start(bf16[1,192,1024]{2,1,0:T(8,128)(2,1)} %param.15) | copy-start | bytes 1179652
  8.0 47.1 %copy-start.8 = (bf16[1,1,192,1024]{3,2,1,0:T(8,128)(2,1)S(1)}, bf16[1,1,192,1024]{3,2,1,0:T(8,128)(2,1)}, u32[]{:S(2)}) copy-start(bf16[1,1,192,1024]{3,2,1,0:T(8,128)(2,1)} %param.11) | copy-start | bytes 1179652
  8.0 47.3 %copy-start.10 = (s32[1,192]{1,0:T(1,128)S(1)}, s32[1,192]{1,0:T(1,128)}, u32[]{:S(2)}) copy-start(s32[1,192]{1,0:T(1,128)} %param.13) | copy-start | bytes 2308
  8.0 83.7 %all-gather.5.cloned.1.call-start = ((), (), s32[]{:S(2)}) async-start(), calls=%async_computation.2 | async-start | bytes 2621440 | tf_op jit(solution)/shard_map/all_gather | solution.py:20
  52.5 862.1 %reduce-scatter.2.cloned.1.call-start = ((), (), s32[]{:S(2)}) async-start(), calls=%async_computation.1 | async-start | bytes 4227072 | tf_op jit(solution)/shard_map/reduce_scatter | solution.py:49
  53.7 4.7 copy-start.6
  55.1 3.3 copy-start.4
  55.4 6.2 copy-start.1
  96.4 3.5 copy-start.2
  101.9 1.8 copy-start.3
  103.6 3.5 copy-start.7
  107.1 8.8 copy-start.5
  122.8 156.2 %copy-start.9 = (bf16[1,192,1024]{2,1,0:T(8,128)(2,1)S(1)}, bf16[1,192,1024]{2,1,0:T(8,128)(2,1)}, u32[]{:S(2)}) copy-start(bf16[1,192,1024]{2,1,0:T(8,128)(2,1)} %param.14) | copy-start | bytes 1179652
  122.8 18.2 %collective-permute-start = (f32[192,1024]{1,0:T(8,128)S(1)}, f32[192,1024]{1,0:T(8,128)S(1)}, u32[]{:S(2)}, u32[]{:S(2)}) collective-permute-start(f32[192,1024]{1,0:T(8,128)S(1)} %get-tuple-element.75), channel_id=1, source_target_pairs={{0,128},{128,256},{256,384},{384,512},{512,640},{1,129},{129,257},... | collective-permute-start | bytes 2359304 | tf_op jit(solution)/shard_map/while/body/eval_jaxpr/ppermute | solution.py:34
  141.2 17.7 %collective-permute-start = (f32[192,1024]{1,0:T(8,128)S(1)}, f32[192,1024]{1,0:T(8,128)S(1)}, u32[]{:S(2)}, u32[]{:S(2)}) collective-permute-start(f32[192,1024]{1,0:T(8,128)S(1)} %get-tuple-element.75), channel_id=1, source_target_pairs={{0,128},{128,256},{256,384},{384,512},{512,640},{1,129},{129,257},... | collective-permute-start | bytes 2359304 | tf_op jit(solution)/shard_map/while/body/eval_jaxpr/ppermute | solution.py:34
  159.0 17.9 %collective-permute-start = (f32[192,1024]{1,0:T(8,128)S(1)}, f32[192,1024]{1,0:T(8,128)S(1)}, u32[]{:S(2)}, u32[]{:S(2)}) collective-permute-start(f32[192,1024]{1,0:T(8,128)S(1)} %get-tuple-element.75), channel_id=1, source_target_pairs={{0,128},{128,256},{256,384},{384,512},{512,640},{1,129},{129,257},... | collective-permute-start | bytes 2359304 | tf_op jit(solution)/shard_map/while/body/eval_jaxpr/ppermute | solution.py:34
  177.0 68.8 %collective-permute-start = (f32[192,1024]{1,0:T(8,128)S(1)}, f32[192,1024]{1,0:T(8,128)S(1)}, u32[]{:S(2)}, u32[]{:S(2)}) collective-permute-start(f32[192,1024]{1,0:T(8,128)S(1)} %get-tuple-element.75), channel_id=1, source_target_pairs={{0,128},{128,256},{256,384},{384,512},{512,640},{1,129},{129,257},... | collective-permute-start | bytes 2359304 | tf_op jit(solution)/shard_map/while/body/eval_jaxpr/ppermute | solution.py:34
  245.9 32.9 %collective-permute-start = (f32[192,1024]{1,0:T(8,128)S(1)}, f32[192,1024]{1,0:T(8,128)S(1)}, u32[]{:S(2)}, u32[]{:S(2)}) collective-permute-start(f32[192,1024]{1,0:T(8,128)S(1)} %get-tuple-element.75), channel_id=1, source_target_pairs={{0,128},{128,256},{256,384},{384,512},{512,640},{1,129},{129,257},... | collective-permute-start | bytes 2359304 | tf_op jit(solution)/shard_map/while/body/eval_jaxpr/ppermute | solution.py:34
Sparse Core Ops, SparseCore 0:
  52.6 39.1 all-gather.4
Sparse Core Ops, SparseCore 1:
  70.3 844.3 reduce-scatter.1
where the time goes:
time: 924 us; the launch traced here: 923 us
  waiting for transfers between devices  699 us (76%)
  starting transfers between devices  113 us (12%)
  blocking collectives  44.4 us (5%)
  matrix products  32.8 us (4%)
  local copies, waits for them, and re-layouts  17.1 us (2%)
  between operations  15.6 us (2%)
    reduce_scatter x1, waiting for transfers between devices, scatter_lines(): lax.psum_scatter(padded.reshape(-1, 128), axis, scatter_dimension=0, tile...  635 us
    ppermute x5, starting transfers between devices, passed_along(): return lax.ppermute(value, axis, pairs)  113 us
    all_gather x2, blocking collectives, stacked_from(): tiles = lax.all_gather(tiles, axes[k])  44.4 us
    ppermute x5, waiting for transfers between devices, passed_along(): return lax.ppermute(value, axis, pairs)  42.2 us
    all_gather x1, waiting for transfers between devices, stacked_from(): tiles = lax.all_gather(tiles, axes[k])  21.6 us
  transfers between devices with their start and end apart: 7, of which 7 were waited for; matrix products, arithmetic and copies ran while one was open for 5% of the time, Pallas kernels for 0%

commit v1 on v0

v1 whole, which is shorter than its diff:
```python
import jax
import jax.numpy as jnp
from jax import lax
from jax.experimental import pallas as pl
from jax.experimental.pallas import tpu as pltpu
from jax.sharding import Mesh
from jax.sharding import PartitionSpec as P

AXES = ("zh", "core", "zl", "y", "x")
AA = ("zh", "core")
BA = ("zl", "y", "x")
SIZE = {"zh": 3, "core": 2, "zl": 4, "y": 8, "x": 4}
MESH = pl.DeviceIdType.MESH
BF = jnp.bfloat16
F32 = jnp.float32
T = 192
D = 1024
PAIRS = 8
HALF = 512
ROWS = 96
COPIES = 128


def mm(a, b, ca, cb):
    return lax.dot_general(a, b, (((ca,), (cb,)), ((), ())), preferred_element_type=F32)


def moved(axis, by):
    n = SIZE[axis]
    return lax.rem(lax.axis_index(axis) + (by % n), n)


class Net:
    def __init__(self, send, recv):
        self.send, self.recv, self.used, self.sent = send, recv, 0, []

    def copy(self, src, dst, axis, by, when=None):
        i = self.used
        self.used += 1
        c = pltpu.make_async_remote_copy(
            src_ref=src,
            dst_ref=dst,
            send_sem=self.send.at[i],
            recv_sem=self.recv.at[i],
            device_id={axis: moved(axis, by)},
            device_id_type=MESH,
        )
        if when is None:
            c.start()
        else:
            pl.when(when)(c.start)
        self.sent.append((c, when))
        return c

    def drain(self):
        for c, when in self.sent:
            if when is None:
                c.wait_send()
            else:
                pl.when(when)(c.wait_send)


def kernel(
    q_hbm, k_hbm, v_hbm, w_hbm, ids_ref, res_hbm, cot_hbm,
    ro_hbm, gq_hbm, gk_hbm, gv_hbm, gp_ref,
    q, k, v, res, cot, wbuf, bias, probs, att, datt, gq, gk, gv, ro,
    prod, y1p, y1m, y1, x1r, x1, z1r, x2r, y2p, y2m, y2s, y2, z2r,
    br, bl, bo, ph, pr,
    in_sem, out_sem, send_sem, recv_sem,
):
    zh, core = lax.axis_index("zh"), lax.axis_index("core")
    z, y, x = (lax.axis_index(a) for a in BA)
    net = Net(send_sem, recv_sem)

    def yy(by):
        return moved("y", by)

    own_w = pltpu.make_async_copy(w_hbm, wbuf.at[z, y, x], in_sem.at[0])
    own_w.start()
    loads = []
    for i, (src, dst) in enumerate(((q_hbm, q), (k_hbm, k), (v_hbm, v), (cot_hbm, cot), (res_hbm, res))):
        c = pltpu.make_async_copy(src, dst, in_sem.at[i + 1])
        c.start()
        loads.append(c)

    barrier = pltpu.get_barrier_semaphore()
    greeted = [("zl", d) for d in (1, 2, 3)] + [("x", d) for d in (1, 2, 3)]
    greeted += [("y", 1), ("y", -1), ("zh", 1), ("zh", 2), ("core", 1)]
    for axis, by in greeted:
        pl.semaphore_signal(barrier, 1, device_id={axis: moved(axis, by)}, device_id_type=MESH)

    ids = jnp.broadcast_to(ids_ref[...], (T, T))
    row = lax.broadcasted_iota(jnp.int32, (T, T), 0)
    lane = lax.broadcasted_iota(jnp.int32, (T, T), 1)
    ids_t = jnp.sum(jnp.where(row == lane, ids, 0).astype(F32), axis=1, keepdims=True)
    bias[...] = jnp.where(jnp.broadcast_to(ids_t, (T, T)) <= ids.astype(F32), 0.0, -1e30)
    first = lax.broadcasted_iota(jnp.int32, (T, 128), 1) < 64

    own_w.wait()
    pl.semaphore_wait(barrier, len(greeted))

    lo, hi = pl.ds(0, HALF), pl.ds(HALF, HALF)

    own = wbuf.at[z, y, x]
    zc = [net.copy(own, own, "zl", d) for d in (1, 2, 3)]

    def halves(val):
        zero = jnp.zeros_like(val)
        return (jnp.where(first, val, zero), jnp.where(first, zero, val))

    def forward(lo_pair, hi_pair):
        def body(h, _):
            sl = pl.ds(pl.multiple_of(h * 128, 128), 128)
            qp = q[:, sl]
            out = jnp.zeros((T, 128), F32)
            for a, (kh, vh) in enumerate(zip(halves(k[:, sl]), halves(v[:, sl]))):
                s = mm(kh, qp, 1, 1) * 0.125 + bias[...]
                e = jnp.exp(s - jnp.max(s, axis=0, keepdims=True))
                p = (e * (1.0 / jnp.sum(e, axis=0, keepdims=True))).astype(BF)
                probs[2 * h + a] = p
                out = out + mm(p, vh, 0, 0)
            att[:, sl] = out.astype(BF)
            return 0

        lax.fori_loop(lo_pair, hi_pair, body, 0)

    def backward(lo_pair, hi_pair):
        def body(h, _):
            sl = pl.ds(pl.multiple_of(h * 128, 128), 128)
            dop = datt[:, sl]
            dv = jnp.zeros((T, 128), F32)
            dk = jnp.zeros((T, 128), F32)
            dq = jnp.zeros((T, 128), F32)
            parts = zip(halves(q[:, sl]), halves(k[:, sl]), halves(v[:, sl]), halves(dop))
            for a, (qh, kh, vh, dh) in enumerate(parts):
                pb = probs[2 * h + a]
                dp = mm(vh, dop, 1, 1)
                p = pb.astype(F32)
                delta = jnp.sum(p * dp, axis=0, keepdims=True)
                ds = (p * (dp - delta) * 0.125).astype(BF)
                dv = dv + mm(pb, dh, 1, 0)
                dk = dk + mm(ds, qh, 1, 0)
                dq = dq + mm(ds, kh, 0, 0)
            gq[:, sl] = dq.astype(BF)
            gk[:, sl] = dk.astype(BF)
            gv[:, sl] = dv.astype(BF)
            return 0

        lax.fori_loop(lo_pair, hi_pair, body, 0)

    for c in loads:
        c.wait()
    forward(0, 2)
    for c in zc:
        c.wait_recv()

    def block(cols, by):
        return wbuf.at[:, yy(by), x, :, cols]

    x1c = [net.copy(block(lo, 0), block(lo, 0), "x", d) for d in (1, 2, 3)]
    x2c = []

    def spread(by):
        for d in (1, 2, 3):
            x2c.append(net.copy(block(hi, by), block(hi, by), "x", d))

    def hop2(t):
        up = net.copy(block(hi, 1 - t), block(hi, 1 - t), "y", 1) if t <= 3 else None
        down = net.copy(block(hi, t - 1), block(hi, t - 1), "y", -1)
        return up, down

    def hop1(t):
        cs = []
        for s in range(2):
            cols = pl.ds(256 * s, 256)
            b = wbuf.at[:, yy(1 - t), :, :, cols]
            cs.append(net.copy(b, b, "y", 1))
            if t <= 3:
                b = wbuf.at[:, yy(t - 1), :, :, cols]
                cs.append(net.copy(b, b, "y", -1))
        return cs

    c2 = hop2(1)
    spread(0)
    forward(2, 4)
    for c in x1c:
        c.wait_recv()
    c1 = hop1(1)
    forward(4, 5)
    for t in range(1, 5):
        up, down = c2
        down.wait_recv()
        if up is not None:
            up.wait_recv()
        if t <= 3:
            c2 = hop2(t + 1)
        if up is not None:
            spread(-t)
        spread(t)
        if t <= 3:
            for c in c1:
                c.wait_recv()
            c1 = hop1(t + 1)
        if t <= 3:
            forward(4 + t, 5 + t)

    for i in range(4):
        pz = mm(att[:, pl.ds(256 * i, 256)], cot[...], 0, 0)
        prod[i] = pz.reshape(8, 4, 8, D).astype(BF)

    def red1(sign, steps, bufs):
        def step(t, got):
            d = yy(sign * (steps + 1 - t))
            cs = []
            for s in range(2):
                cols = pl.ds(256 * s, 256)
                if t == 1:
                    src = prod.at[:, d, :, :, cols]
                else:
                    got[s].wait_recv()
                    src = bufs.at[t - 2, :, :, :, cols]
                    total = src[...].astype(F32) + prod[:, d, :, :, cols].astype(F32)
                    bufs[t - 2, :, :, :, cols] = total.astype(BF)
                cs.append(net.copy(src, bufs.at[t - 1, :, :, :, cols], "y", sign))
            return cs

        return step

    up1, down1 = red1(1, 4, y1p), red1(-1, 3, y1m)
    u1, d1 = up1(1, None), down1(1, None)

    x2sent = {}
    for by in (-4, 3, -3, 2, -2, 1, -1, 0):
        d = yy(by)
        x2sent[by] = [
            net.copy(prod.at[:, d, moved("x", dx), :, hi], x2r.at[dx - 1, :, d], "x", dx) for dx in (1, 2, 3)
        ]

    def x2sum(by):
        for c in x2sent[by]:
            c.wait_recv()
        d = yy(by)
        total = prod[:, d, x, :, hi].astype(F32)
        for j in range(3):
            total = total + x2r[j, :, d].astype(F32)
        return total

    for c in c1 + x2c:
        c.wait_recv()

    w_all = wbuf[...].reshape(D, D)
    a_all = att[...]
    other = pl.ds(0, T)
    swaps = []
    for h in range(2):
        cols = pl.ds(HALF * h, HALF)
        b = mm(a_all, w_all[:, HALF * h : HALF * h + HALF], 1, 0)
        br[:, cols] = b
        bl[:, cols] = b.astype(BF)
        swaps.append(net.copy(bl.at[:, cols], bo.at[:, cols], "core", 1))
    datt[...] = mm(cot[...], w_all, 1, 1).astype(BF)
    mine = pl.ds(pl.multiple_of(core * ROWS, 8), ROWS)
    far = []
    for h in range(2):
        cols = pl.ds(HALF * h, HALF)
        swaps[h].wait_recv()
        ph[:, cols] = (br[mine, cols] + bo[mine, cols].astype(F32)).astype(BF)
        near = net.copy(ph.at[:, cols], pr.at[0, mine, cols], "zh", 1, when=zh < 2)
        skip = net.copy(ph.at[:, cols], pr.at[1, mine, cols], "zh", 2, when=zh == 0)
        far.append((near, skip))

    def up2(t, got):
        d = 4 - t
        total = x2sum(d)
        if t > 1:
            got.wait_recv()
            total = total + y2p[t - 2].astype(F32)
        y2s[t - 1] = total.astype(BF)
        return net.copy(y2s.at[t - 1], y2p.at[t - 1], "y", 1)

    def down2(t, got):
        d = t - 5
        total = x2sum(d)
        if t > 1:
            got.wait_recv()
            total = total + y2m[t - 2].astype(F32)
        y2s[2 + t] = total.astype(BF)
        return net.copy(y2s.at[2 + t], y2m.at[t - 1], "y", -1)

    u2 = d2 = None
    for t in range(1, 5):
        d2 = down2(t, d2)
        if t <= 3:
            u2 = up2(t, u2)
        if t <= 3:
            u1 = up1(t + 1, u1)
        if t <= 2:
            d1 = down1(t + 1, d1)
        backward(2 * t - 2, 2 * t)
    outs = []

    def store(i, src, dst):
        c = pltpu.make_async_copy(src, dst, out_sem.at[i])
        c.start()
        outs.append(c)

    store(0, gq, gq_hbm)
    store(1, gk, gk_hbm)
    store(2, gv, gv_hbm)

    for c in u1 + d1:
        c.wait_recv()
    y1[...] = (prod[:, y, :, :, lo].astype(F32) + y1p[3].astype(F32) + y1m[2].astype(F32)).astype(BF)
    x1c = [net.copy(y1.at[:, moved("x", dx)], x1r.at[dx - 1], "x", dx) for dx in (1, 2, 3)]

    total = x2sum(0)
    u2.wait_recv()
    d2.wait_recv()
    total = total + y2p[2].astype(F32) + y2m[3].astype(F32)
    y2[...] = total.astype(BF)
    z2c = [net.copy(y2.at[moved("zl", dz)], z2r.at[dz - 1], "zl", dz) for dz in (1, 2, 3)]

    for c in x1c:
        c.wait_recv()
    total = y1[:, x].astype(F32)
    for j in range(3):
        total = total + x1r[j].astype(F32)
    x1[...] = total.astype(BF)
    z1c = [net.copy(x1.at[moved("zl", dz)], z1r.at[dz - 1], "zl", dz) for dz in (1, 2, 3)]

    for cols, last, sums, got in ((hi, y2, z2r, z2c), (lo, x1, z1r, z1c)):
        for c in got:
            c.wait_recv()
        total = last[z].astype(F32)
        for j in range(3):
            total = total + sums[j].astype(F32)
        gp_ref[:, cols] = total * (1.0 / 128.0)

    passed = []
    for h in range(2):
        cols = pl.ds(HALF * h, HALF)
        near, skip = far[h]
        pl.when(zh > 0)(near.wait_recv)
        a = pr.at[0, mine, cols]
        passed.append((net.copy(a, a, "core", 1, when=zh > 0), zh > 0))
        pl.when(zh == 2)(skip.wait_recv)
        a = pr.at[1, mine, cols]
        passed.append((net.copy(a, a, "core", 1, when=zh == 2), zh == 2))
    br[...] = br[...] + res[...].astype(F32)

    @pl.when(core == 1)
    def _():
        br[...] = br[...] + bo[...].astype(F32)

    for c, when in passed:
        pl.when(when)(c.wait_recv)

    @pl.when(zh > 0)
    def _():
        br[...] = br[...] + pr[0].astype(F32)

    @pl.when(zh == 2)
    def _():
        br[...] = br[...] + pr[1].astype(F32)

    ro[...] = br[...].astype(BF)
    store(3, ro, ro_hbm)
    net.drain()
    for c in outs:
        c.wait()


def local(queries, key_rows, value_rows, out_proj, scale_ids, residual_in, cotangent):
    anyspace = pl.BlockSpec(memory_space=pl.ANY)
    vmem = pl.BlockSpec(memory_space=pltpu.VMEM)
    act = jax.ShapeDtypeStruct((T, D), BF)
    V = pltpu.VMEM
    scratch = [V((T, D), BF)] * 5 + [
        V((4, 8, 4, 8, D), BF),
        V((T, T), F32),
        V((16, T, T), BF),
    ] + [V((T, D), BF)] * 6 + [
        V((4, 8, 4, 8, D), BF),
        V((4, 4, 4, 8, HALF), BF),
        V((3, 4, 4, 8, HALF), BF),
        V((4, 4, 8, HALF), BF),
        V((3, 4, 8, HALF), BF),
        V((4, 8, HALF), BF),
        V((3, 8, HALF), BF),
        V((3, 4, 8, 8, HALF), BF),
        V((3, 4, 8, HALF), BF),
        V((4, 4, 8, HALF), BF),
        V((7, 4, 8, HALF), BF),
        V((4, 8, HALF), BF),
        V((3, 8, HALF), BF),
        V((T, D), F32),
        V((T, D), BF),
        V((T, D), BF),
        V((ROWS, D), BF),
        V((2, T, D), BF),
        pltpu.SemaphoreType.DMA((6,)),
        pltpu.SemaphoreType.DMA((4,)),
        pltpu.SemaphoreType.DMA((COPIES,)),
        pltpu.SemaphoreType.DMA((COPIES,)),
    ]
    ro, gq, gk, gv, gp = pl.pallas_call(
        kernel,
        out_shape=(act, act, act, act, jax.ShapeDtypeStruct((8, D), F32)),
        in_specs=[anyspace] * 4 + [vmem] + [anyspace] * 2,
        out_specs=(anyspace, anyspace, anyspace, anyspace, vmem),
        scratch_shapes=scratch,
        compiler_params=pltpu.CompilerParams(
            collective_id=0, has_side_effects=True, vmem_limit_bytes=56 << 20
        ),
        name="fused",
    )(
        queries.reshape(T, D), key_rows.reshape(T, D), value_rows.reshape(T, D), out_proj.reshape(8, D),
        scale_ids, residual_in.reshape(T, D), cotangent.reshape(T, D),
    )
    lead = (1, 1, T, D)
    return ro.reshape(lead), gq.reshape(lead), gk.reshape(lead), gv.reshape(lead), gp.reshape(1, 8, D)


def solution(mesh):
    torus = Mesh(mesh.devices.reshape(tuple(SIZE[a] for a in AXES)), AXES)
    act = P(AA, BA, None, None)
    return jax.shard_map(
        local,
        mesh=torus,
        in_specs=(act, act, act, P(AA, BA, None), P(BA, None), P(BA, None, None), P(BA, None, None)),
        out_specs=(act, act, act, act, P(AA, BA, None)),
        check_vma=False,
    )
```

time: 924 us -> 80.4 us (0.09)
  the two profiles are of different devices: /device:TPU:256 before, /device:TPU:1 now
where the time goes in v1:
time: 80.4 us; the launch traced here: 79.3 us
  Pallas kernels  73.2 us (91%)
  local copies, waits for them, and re-layouts  5.47 us (7%)
    pallas_call x1, Pallas kernels, local(): pl.pallas_call(kernel, out_shape=(act, act, act, act, jax.ShapeDtypeStruc...  73.2 us
    unnamed x13, local copies, waits for them, and re-layouts  5.47 us

profile of v1, /device:TPU:1, one launch (start us, length us, event | category | flops | bytes accessed | tf_op | source)
XLA Modules:
  0.0 79.3 jit_solution(3503021776644143307)
XLA Ops:
  0.6 73.2 %fused.1 = (bf16[192,1024]{1,0:T(8,128)(2,1)}, bf16[192,1024]{1,0:T(8,128)(2,1)}, bf16[192,1024]{1,0:T(8,128)(2,1)}, bf16[192,1024]{1,0:T(8,128)(2,1)}, f32[8,1024]{1,0:T(8,128)}) custom-call(bf16[192,1024]{1,0:T(8,128)(2,1)} %bitcast.11, bf16[192,1024]{1,0:T(8,128)(2,1)} %bitcast.12, bf16[192,1024]{1,0:T(8,128)(2,1)} %bitcast.13, bf16[8,1024]{1,0:T(8,128)(2,1)} %bitcast.21, ...), custom_call_target="tpu_custom_call" | custom-call | tf_op jit(solution)/shard_map/fused/pallas_call | solution.py:406
  73.8 0.0 copy-start.2
  73.8 1.8 %copy.17 = bf16[1,1,192,1024]{3,2,1,0:T(8,128)(2,1)} copy(bf16[1,1,192,1024]{3,2,1,0:T(8,128)(2,1)} %bitcast.19) | data formatting | bytes 786432
  75.7 0.0 copy-done.2
  75.7 0.0 copy-start.1
  75.7 0.7 copy.18
  76.4 0.4 copy-done.1
  76.8 0.0 copy-start
  76.8 0.7 copy.19
  77.6 0.4 copy-done
  77.9 0.0 copy-start.3
  77.9 0.7 copy.20
  78.7 0.0 copy-done.3
  78.7 0.6 copy.21
Async XLA Ops:
  73.8 1.8 %copy-start.2 = (bf16[192,1024]{1,0:T(8,128)(2,1)S(1)}, bf16[192,1024]{1,0:T(8,128)(2,1)}, u32[]{:S(2)}) copy-start(bf16[192,1024]{1,0:T(8,128)(2,1)} %get-tuple-element.11) | copy-start | bytes 1179652
  75.7 1.1 %copy-start.1 = (bf16[192,1024]{1,0:T(8,128)(2,1)S(1)}, bf16[192,1024]{1,0:T(8,128)(2,1)}, u32[]{:S(2)}) copy-start(bf16[192,1024]{1,0:T(8,128)(2,1)} %get-tuple-element.12) | copy-start | bytes 1179652
  76.8 1.1 %copy-start = (bf16[192,1024]{1,0:T(8,128)(2,1)S(1)}, bf16[192,1024]{1,0:T(8,128)(2,1)}, u32[]{:S(2)}) copy-start(bf16[192,1024]{1,0:T(8,128)(2,1)} %get-tuple-element.13) | copy-start | bytes 1179652
  77.9 0.8 copy-start.3

commit v2 on v1

--- a/solution.py
+++ b/solution.py
@@ -18,7 +18,7 @@
 PAIRS = 8
 HALF = 512
 ROWS = 96
-COPIES = 128
+COPIES = 144
 
 
 def mm(a, b, ca, cb):
@@ -62,11 +62,11 @@
 
 def kernel(
     q_hbm, k_hbm, v_hbm, w_hbm, ids_ref, res_hbm, cot_hbm,
-    ro_hbm, gq_hbm, gk_hbm, gv_hbm, gp_ref,
-    q, k, v, res, cot, wbuf, bias, probs, att, datt, gq, gk, gv, ro,
+    ro, gq, gk, gv, gp_ref,
+    q, k, v, res, cot, wbuf, bias, probs, att, datt,
     prod, y1p, y1m, y1, x1r, x1, z1r, x2r, y2p, y2m, y2s, y2, z2r,
     br, bl, bo, ph, pr,
-    in_sem, out_sem, send_sem, recv_sem,
+    in_sem, send_sem, recv_sem, ready,
 ):
     zh, core = lax.axis_index("zh"), lax.axis_index("core")
     z, y, x = (lax.axis_index(a) for a in BA)
@@ -85,9 +85,15 @@
 
     barrier = pltpu.get_barrier_semaphore()
     greeted = [("zl", d) for d in (1, 2, 3)] + [("x", d) for d in (1, 2, 3)]
-    greeted += [("y", 1), ("y", -1), ("zh", 1), ("zh", 2), ("core", 1)]
+    greeted += [("y", 1), ("y", -1), ("core", 1)]
+
+    def signal(sem, axis, by):
+        pl.semaphore_signal(sem, 1, device_id={axis: moved(axis, by)}, device_id_type=MESH)
+
     for axis, by in greeted:
-        pl.semaphore_signal(barrier, 1, device_id={axis: moved(axis, by)}, device_id_type=MESH)
+        signal(barrier, axis, by)
+    pl.when(zh < 2)(lambda: signal(barrier, "zh", 1))
+    pl.when(zh == 0)(lambda: signal(barrier, "zh", 2))
 
     ids = jnp.broadcast_to(ids_ref[...], (T, T))
     row = lax.broadcasted_iota(jnp.int32, (T, T), 0)
@@ -97,7 +103,9 @@
     first = lax.broadcasted_iota(jnp.int32, (T, 128), 1) < 64
 
     own_w.wait()
-    pl.semaphore_wait(barrier, len(greeted))
+    pl.semaphore_wait(barrier, len(greeted) + zh)
+    pl.when(zh > 0)(lambda: signal(ready.at[0], "zh", -1))
+    pl.when(zh == 2)(lambda: signal(ready.at[1], "zh", -2))
 
     lo, hi = pl.ds(0, HALF), pl.ds(HALF, HALF)
 
@@ -169,15 +177,21 @@
         down = net.copy(block(hi, t - 1), block(hi, t - 1), "y", -1)
         return up, down
 
-    def hop1(t):
-        cs = []
-        for s in range(2):
-            cols = pl.ds(256 * s, 256)
-            b = wbuf.at[:, yy(1 - t), :, :, cols]
-            cs.append(net.copy(b, b, "y", 1))
-            if t <= 3:
-                b = wbuf.at[:, yy(t - 1), :, :, cols]
-                cs.append(net.copy(b, b, "y", -1))
+    def hop1(t, got):
+        cs = {}
+        for s in range(4):
+            cols = pl.ds(128 * s, 128)
+            for sign in (1, -1):
+                if t == 4 and (s < 2) != (sign == 1):
+                    continue
+                if got is not None:
+                    got[sign, s].wait_recv()
+                b = wbuf.at[:, yy(sign * (1 - t)), :, :, cols]
+                cs[sign, s] = net.copy(b, b, "y", sign)
+        if got is not None:
+            for key in got:
+                if key not in cs:
+                    got[key].wait_recv()
         return cs
 
     c2 = hop2(1)
@@ -185,7 +199,7 @@
     forward(2, 4)
     for c in x1c:
         c.wait_recv()
-    c1 = hop1(1)
+    c1 = hop1(1, None)
     forward(4, 5)
     for t in range(1, 5):
         up, down = c2
@@ -198,9 +212,7 @@
             spread(-t)
         spread(t)
         if t <= 3:
-            for c in c1:
-                c.wait_recv()
-            c1 = hop1(t + 1)
+            c1 = hop1(t + 1, c1)
         if t <= 3:
             forward(4 + t, 5 + t)
 
@@ -245,7 +257,7 @@
             total = total + x2r[j, :, d].astype(F32)
         return total
 
-    for c in c1 + x2c:
+    for c in list(c1.values()) + x2c:
         c.wait_recv()
 
     w_all = wbuf[...].reshape(D, D)
@@ -261,6 +273,8 @@
     datt[...] = mm(cot[...], w_all, 1, 1).astype(BF)
     mine = pl.ds(pl.multiple_of(core * ROWS, 8), ROWS)
     far = []
+    pl.when(zh < 2)(lambda: pl.semaphore_wait(ready.at[0], 1))
+    pl.when(zh == 0)(lambda: pl.semaphore_wait(ready.at[1], 1))
     for h in range(2):
         cols = pl.ds(HALF * h, HALF)
         swaps[h].wait_recv()
@@ -297,17 +311,6 @@
         if t <= 2:
             d1 = down1(t + 1, d1)
         backward(2 * t - 2, 2 * t)
-    outs = []
-
-    def store(i, src, dst):
-        c = pltpu.make_async_copy(src, dst, out_sem.at[i])
-        c.start()
-        outs.append(c)
-
-    store(0, gq, gq_hbm)
-    store(1, gk, gk_hbm)
-    store(2, gv, gv_hbm)
-
     for c in u1 + d1:
         c.wait_recv()
     y1[...] = (prod[:, y, :, :, lo].astype(F32) + y1p[3].astype(F32) + y1m[2].astype(F32)).astype(BF)
@@ -364,9 +367,15 @@
         br[...] = br[...] + pr[1].astype(F32)
 
     ro[...] = br[...].astype(BF)
-    store(3, ro, ro_hbm)
     net.drain()
-    for c in outs:
+
+
+def write_out(*refs):
+    sem = refs[10]
+    copies = [pltpu.make_async_copy(refs[i], refs[5 + i], sem.at[i]) for i in range(5)]
+    for c in copies:
+        c.start()
+    for c in copies:
         c.wait()
 
 
@@ -379,7 +388,7 @@
         V((4, 8, 4, 8, D), BF),
         V((T, T), F32),
         V((16, T, T), BF),
-    ] + [V((T, D), BF)] * 6 + [
+    ] + [V((T, D), BF)] * 2 + [
         V((4, 8, 4, 8, D), BF),
         V((4, 4, 4, 8, HALF), BF),
         V((3, 4, 4, 8, HALF), BF),
@@ -399,15 +408,16 @@
         V((ROWS, D), BF),
         V((2, T, D), BF),
         pltpu.SemaphoreType.DMA((6,)),
-        pltpu.SemaphoreType.DMA((4,)),
         pltpu.SemaphoreType.DMA((COPIES,)),
         pltpu.SemaphoreType.DMA((COPIES,)),
+        pltpu.SemaphoreType.REGULAR((2,)),
     ]
-    ro, gq, gk, gv, gp = pl.pallas_call(
+    held = (V((T, D), BF),) * 4 + (V((8, D), F32),)
+    made = pl.pallas_call(
         kernel,
-        out_shape=(act, act, act, act, jax.ShapeDtypeStruct((8, D), F32)),
+        out_shape=held,
         in_specs=[anyspace] * 4 + [vmem] + [anyspace] * 2,
-        out_specs=(anyspace, anyspace, anyspace, anyspace, vmem),
+        out_specs=(vmem,) * 5,
         scratch_shapes=scratch,
         compiler_params=pltpu.CompilerParams(
             collective_id=0, has_side_effects=True, vmem_limit_bytes=56 << 20
@@ -417,6 +427,14 @@
         queries.reshape(T, D), key_rows.reshape(T, D), value_rows.reshape(T, D), out_proj.reshape(8, D),
         scale_ids, residual_in.reshape(T, D), cotangent.reshape(T, D),
     )
+    ro, gq, gk, gv, gp = pl.pallas_call(
+        write_out,
+        out_shape=(act, act, act, act, jax.ShapeDtypeStruct((8, D), F32)),
+        in_specs=[vmem] * 5,
+        out_specs=(anyspace,) * 5,
+        scratch_shapes=[pltpu.SemaphoreType.DMA((5,))],
+        name="write_out",
+    )(*(pltpu.with_memory_space_constraint(a, pltpu.VMEM) for a in made))
     lead = (1, 1, T, D)
     return ro.reshape(lead), gq.reshape(lead), gk.reshape(lead), gv.reshape(lead), gp.reshape(1, 8, D)
 

time: 80.4 us -> 67.4 us (0.84)
  the two profiles are of different devices: /device:TPU:1 before, /device:TPU:257 now
where the time goes in v2:
time: 67.4 us; the launch traced here: 67.2 us
  Pallas kernels  66.5 us (99%)
    pallas_call x1, Pallas kernels, local(): pl.pallas_call(kernel, out_shape=held, in_specs=[anyspace] * 4 + [vmem] +...  65.3 us

profile of v2, /device:TPU:257, one launch (start us, length us, event | category | flops | bytes accessed | tf_op | source)
XLA Modules:
  0.0 67.2 jit_solution(16213211350625698086)
XLA Ops:
  0.6 65.3 %fused.1 = (bf16[192,1024]{1,0:T(8,128)(2,1)S(1)}, bf16[192,1024]{1,0:T(8,128)(2,1)S(1)}, bf16[192,1024]{1,0:T(8,128)(2,1)S(1)}, bf16[192,1024]{1,0:T(8,128)(2,1)S(1)}, f32[8,1024]{1,0:T(8,128)S(1)}) custom-call(bf16[192,1024]{1,0:T(8,128)(2,1)} %bitcast.11, bf16[192,1024]{1,0:T(8,128)(2,1)} %bitcast.12, bf16[192,1024]{1,0:T(8,128)(2,1)} %bitcast.13, ...), custom_call_target="tpu_custom_call" | custom-call | tf_op jit(solution)/shard_map/fused/pallas_call | solution.py:416
  66.0 1.2 %write_out.1 = (bf16[192,1024]{1,0:T(8,128)(2,1)}, bf16[192,1024]{1,0:T(8,128)(2,1)}, bf16[192,1024]{1,0:T(8,128)(2,1)}, bf16[192,1024]{1,0:T(8,128)(2,1)}, f32[8,1024]{1,0:T(8,128)}) custom-call(bf16[192,1024]{1,0:T(8,128)(2,1)S(1)} %get-tuple-element.15.refs_0_, bf16[192,1024]{1,0:T(8,128)(2,1)S(1)} %get-tuple-element.16.refs_1_, ...), custom_call_target="tpu_custom_call" | custom-call | tf_op jit(solution)/shard_map/write_out/pallas_call | solution.py:430
